TPU v7x, 32 devices: a whole 2x2x4 slice. The times are simulated.
32 devices in a mesh: probe: 4 (over y, x), space: 8 (over z, core).
Axes of the slice: x: 2, y: 2, z: 4, core: 2. Of those that a mesh axis runs over, the one named last changes fastest.
Arguments:
- probe_signs: int32 [192, 64, 1024], P('probe', 'space'), may hold values from 0 to 1, as said below
- sensor_mask: int32 [64, 1024], P('space'), may hold values 0 or 1
- sensor_weight: float32 [64, 1024], P('space'), may hold values from 1 to 30
- prior_mass: float32 [64, 1024], P('space'), may hold values from 0.02 to 0.5
Outputs:
- solution: float32 [192, 64, 1024], P('probe', 'space')
- trace_cell: float32 [], replicated
Inputs may be any that keep to these rules, and one draw needn't show every extreme that they name: `probe_signs`: each entry is 0 or 1; the probe's sign is twice the entry minus one.
All inputs are finite; a program needn't handle non-finite values. No bound on the sum of `sensor_mask` on one device may be relied on, other than what follows from the above.
Results may differ from a plain program's by a relative error of at most 0.0001.
Values sent between devices are 32-bit elements; how exact they have to be, the bound alone decides.
A program may use at most 64 MiB of HBM per device.

v0:
```python
import jax
import jax.numpy as jnp
from jax import lax
from jax.sharding import PartitionSpec as P

ITERS = 4


def with_halo(cells, sides, width):
    for axis, dim in sides:
        count = lax.axis_size(axis)
        ends = count - 1
        head = lax.slice_in_dim(cells, 0, width, axis=dim)
        tail = lax.slice_in_dim(cells, cells.shape[dim] - width, cells.shape[dim], axis=dim)
        cells = jnp.concatenate(
            [
                lax.ppermute(tail, axis, [(i, (i + 1) % count) for i in range(ends)]),
                cells,
                lax.ppermute(head, axis, [((i + 1) % count, i) for i in range(ends)]),
            ],
            axis=dim,
        )
    return cells


def operate(vector_in, diagonal):
    padded = with_halo(vector_in, (("space", 1),), 1)
    padded = jnp.pad(padded, ((0, 0), (0, 0), (1, 1)))
    beside = padded[:, 2:, 1:-1] + padded[:, :-2, 1:-1]
    beside = beside + padded[:, 1:-1, 2:] + padded[:, 1:-1, :-2]
    return (4.0 + diagonal) * vector_in - beside


def per_probe(values):
    return jnp.sum(values, axis=(1, 2))


def two_sums(residual, applied):
    return lax.psum((per_probe(residual * residual), per_probe(residual * applied)), "space")


def on_device(probe_signs, sensor_mask, sensor_weight, prior_mass):
    probes = 2.0 * probe_signs.astype(jnp.float32) - 1.0
    diagonal = sensor_mask.astype(jnp.float32) * sensor_weight + prior_mass
    solution = jnp.zeros_like(probes)
    residual = probes
    applied = operate(residual, diagonal)
    norm_now, curvature = two_sums(residual, applied)
    step_len = norm_now / curvature
    direction = residual
    applied_dir = applied
    for iterate in range(ITERS):
        solution = solution + step_len[:, None, None] * direction
        residual = residual - step_len[:, None, None] * applied_dir
        if iterate + 1 < ITERS:
            applied = operate(residual, diagonal)
            norm_next, curvature = two_sums(residual, applied)
            step_ratio = norm_next / norm_now
            step_len = norm_next / (curvature - step_ratio * norm_next / step_len)
            direction = residual + step_ratio[:, None, None] * direction
            applied_dir = applied + step_ratio[:, None, None] * applied_dir
            norm_now = norm_next
    local_part = jnp.sum(probes * solution)
    trace_sum = lax.psum(local_part, ("probe", "space"))
    cells = (
        probes.shape[0]
        * lax.axis_size("probe")
        * probes.shape[1]
        * lax.axis_size("space")
        * probes.shape[2]
    )
    return (solution, trace_sum / float(cells))


def solution(mesh):
    return jax.shard_map(
        on_device,
        mesh=mesh,
        in_specs=(P("probe", "space", None), P("space", None), P("space", None), P("space", None)),
        out_specs=(P("probe", "space", None), P()),
        check_vma=False,
    )
```

profile of v0, /device:TPU:0, one launch (start us, length us, event | category | flops | bytes accessed | tf_op | source)
XLA Modules:
  0.0 160.7 jit_solution(1238843846000339641)
XLA Ops:
  0.7 2.5 %fusion.12 = f32[48,8,1024]{2,0,1:T(8,128)S(1)} fusion(s32[48,8,1024]{2,1,0:T(8,128)} %param.4), kind=kLoop, calls=%fused_computation.39 | loop fusion | flops 1179648 | bytes 3145728 | tf_op jit(solution)/shard_map/sub | solution.py:43
  3.2 2.4 %collective-permute-start.1 = (f32[48,1,1024]{2,0,1:T(8,128)S(1)}, f32[48,1,1024]{2,0,1:T(8,128)S(1)}, u32[]{:S(2)}, u32[]{:S(2)}) collective-permute-start(f32[48,1,1024]{2,0,1:T(8,128)S(1)} %get-tuple-element.38), channel_id=1, source_target_pairs={{0,1},{1,2},{2,3},{3,4},{4,5},{5,6},{6,7},{8,9},{9,10},{10,11},{11... | collective-permute-start | bytes 589832 | tf_op jit(solution)/shard_map/ppermute | solution.py:17
  5.6 1.3 collective-permute-start
  7.0 4.1 %collective-permute-done = f32[48,1,1024]{2,0,1:T(8,128)S(1)} collective-permute-done((f32[48,1,1024]{2,0,1:T(8,128)S(1)}, f32[48,1,1024]{2,0,1:T(8,128)S(1)}, u32[]{:S(2)}, u32[]{:S(2)}) %collective-permute-start) | collective-permute-done | bytes 196640 | tf_op jit(solution)/shard_map/ppermute | solution.py:19
  11.8 2.8 %multiply_reduce_fusion.6 = (f32[48]{0:T(128)S(1)}, f32[48]{0:T(128)S(1)}, f32[48,8,1024]{2,0,1:T(8,128)}) fusion(s32[48,8,1024]{2,1,0:T(8,128)S(1)} %copy-done.2, f32[48,10,1026]{2,0,1:T(8,128)S(1)} %select_maximum_fusion.6, f32[48,8,1024]{2,0,1:T(8,128)S(1)} %fusion.12, f32[48,1,1024]{2,0,1:T(8,128)S(1)} %collective-permute-done.1, ...), kind=kLoop, calls=%fused_computation.51 | loop fusion | flops 5504928 | bytes 8290688 | tf_op jit(solution)/shard_map/reduce_sum | solution.py:35
  14.6 17.7 %all-reduce.7 = (f32[48]{0:T(128)S(1)}, f32[48]{0:T(128)S(1)}) all-reduce(f32[48]{0:T(128)S(1)} %get-tuple-element.11, f32[48]{0:T(128)S(1)} %get-tuple-element.10), channel_id=1, replica_groups=mesh['probe'=4,'space'=8] {'space'}, use_global_device_ids=true, to_apply=%region_1.2 | all-reduce | flops 96 | bytes 768 | tf_op jit(solution)/shard_map/psum | solution.py:39
  32.3 2.6 %multiply_subtract_fusion.2 = f32[48,8,1024]{2,0,1:T(8,128)S(1)} fusion(f32[48,8,1024]{2,0,1:T(8,128)} %get-tuple-element.31, f32[48]{0:T(128)S(1)} %div.33, s32[48,8,1024]{2,1,0:T(8,128)S(1)} %copy-done.2), kind=kLoop, calls=%fused_computation.50 | loop fusion | flops 1966080 | bytes 4718784 | tf_op jit(solution)/shard_map/sub | solution.py:54
  35.0 1.3 collective-permute-start.3
  36.3 1.3 collective-permute-start.2
  37.6 2.0 %collective-permute-done.2 = f32[48,1,1024]{2,0,1:T(8,128)S(1)} collective-permute-done((f32[48,1,1024]{2,0,1:T(8,128)S(1)}, f32[48,1,1024]{2,0,1:T(8,128)S(1)}, u32[]{:S(2)}, u32[]{:S(2)}) %collective-permute-start.2) | collective-permute-done | bytes 196640 | tf_op jit(solution)/shard_map/ppermute | solution.py:19
  40.3 2.0 %multiply_reduce_fusion.4 = (f32[48]{0:T(128)S(1)}, f32[48]{0:T(128)S(1)}, f32[48,8,1024]{2,0,1:T(8,128)}) fusion(f32[48,8,1024]{2,0,1:T(8,128)S(1)} %multiply_subtract_fusion.2, f32[48,10,1026]{2,0,1:T(8,128)S(1)} %select_maximum_fusion.4, f32[48,1,1024]{2,0,1:T(8,128)S(1)} %collective-permute-done.3, f32[48,1,1024]{2,0,1:T(8,128)S(1)} %collective-permute-done.2, ...), kind=kLoop, calls=%fused_computation.48 | loop fusion | flops 4325280 | bytes 6717824 | tf_op jit(solution)/shard_map/reduce_sum | solution.py:35
  42.3 16.2 %all-reduce.6 = (f32[48]{0:T(128)S(1)}, f32[48]{0:T(128)S(1)}) all-reduce(f32[48]{0:T(128)S(1)} %get-tuple-element.9, f32[48]{0:T(128)S(1)} %get-tuple-element.8), channel_id=1, replica_groups=mesh['probe'=4,'space'=8] {'space'}, use_global_device_ids=true, to_apply=%region_5.6 | all-reduce | flops 96 | bytes 768 | tf_op jit(solution)/shard_map/psum | solution.py:39
  59.0 2.4 %multiply_subtract_fusion.1 = f32[48,8,1024]{2,0,1:T(8,128)S(1)} fusion(f32[48,8,1024]{2,0,1:T(8,128)S(1)} %multiply_subtract_fusion.2, f32[48]{0:T(128)S(1)} %get-tuple-element.27, f32[48,8,1024]{2,0,1:T(8,128)} %get-tuple-element.30, f32[48,8,1024]{2,0,1:T(8,128)} %get-tuple-element.31, f32[48]{0:T(128)S(1)} %get-tuple-element.29), kind=kLoop, calls=%fused_computation.46 | loop fusion | flops 1572864 | bytes 6291840 | tf_op jit(solution)/shard_map/sub | solution.py:54
  61.5 1.3 collective-permute-start.5
  64.1 2.0 %collective-permute-done.4 = f32[48,1,1024]{2,0,1:T(8,128)S(1)} collective-permute-done((f32[48,1,1024]{2,0,1:T(8,128)S(1)}, f32[48,1,1024]{2,0,1:T(8,128)S(1)}, u32[]{:S(2)}, u32[]{:S(2)}) %collective-permute-start.4) | collective-permute-done | bytes 196640 | tf_op jit(solution)/shard_map/ppermute | solution.py:19
  68.2 16.6 %all-reduce.5 = (f32[48]{0:T(128)}, f32[48]{0:T(128)}) all-reduce(f32[48]{0:T(128)S(1)} %get-tuple-element.7, f32[48]{0:T(128)S(1)} %get-tuple-element.6), channel_id=1, replica_groups=mesh['probe'=4,'space'=8] {'space'}, use_global_device_ids=true, to_apply=%region_9.10 | all-reduce | flops 96 | bytes 768 | tf_op jit(solution)/shard_map/psum | solution.py:39
  86.0 3.9 %multiply_subtract_fusion = f32[48,8,1024]{2,0,1:T(8,128)S(1)} fusion(f32[48,8,1024]{2,0,1:T(8,128)S(1)} %multiply_subtract_fusion.1, f32[48]{0:T(128)S(1)} %get-tuple-element.26, f32[48]{0:T(128)S(1)} %get-tuple-element.24, f32[48,8,1024]{2,0,1:T(8,128)} %get-tuple-element.30, f32[48,8,1024]{2,0,1:T(8,128)} %get-tuple-element.31, ...), kind=kLoop, calls=%fused_computation.43 | loop fusion | flops 5111808 | bytes 9863744 | tf_op jit(solution)/shard_map/sub | solution.py:54
  90.0 1.3 collective-permute-start.7
  91.3 1.3 collective-permute-start.6
  92.6 2.0 %collective-permute-done.6 = f32[48,1,1024]{2,0,1:T(8,128)S(1)} collective-permute-done((f32[48,1,1024]{2,0,1:T(8,128)S(1)}, f32[48,1,1024]{2,0,1:T(8,128)S(1)}, u32[]{:S(2)}, u32[]{:S(2)}) %collective-permute-start.6) | collective-permute-done | bytes 196640 | tf_op jit(solution)/shard_map/ppermute | solution.py:19
  96.1 16.2 %all-reduce.4 = (f32[48]{0:T(128)S(1)}, f32[48]{0:T(128)S(1)}) all-reduce(f32[48]{0:T(128)S(1)} %get-tuple-element.5, f32[48]{0:T(128)S(1)} %get-tuple-element.4), channel_id=1, replica_groups=mesh['probe'=4,'space'=8] {'space'}, use_global_device_ids=true, to_apply=%region_13.14 | all-reduce | flops 96 | bytes 768 | tf_op jit(solution)/shard_map/psum | solution.py:39
  112.3 5.1 %multiply_reduce_fusion = (f32[]{:T(128)}, f32[48,8,1024]{2,0,1:T(8,128)}) fusion(s32[48,8,1024]{2,1,0:T(8,128)} %param.4, f32[48,8,1024]{2,0,1:T(8,128)} %copy-done.1, f32[48]{0:T(128)S(1)} %get-tuple-element.23, f32[48]{0:T(128)S(1)} %get-tuple-element.22, f32[48,8,1024]{2,0,1:T(8,128)S(1)} %multiply_subtract_fusion.1, f32[48]{0:T(128)S(1)} %get-tuple-element.26, ...), kind=kLoop, calls=%fused_computation.40 | loop fusion | flops 7077887 | bytes 7865668 | tf_op jit(solution)/shard_map/reduce_sum | solution.py:63
  117.4 38.0 %psum.71 = f32[]{:T(128)} all-reduce(f32[]{:T(128)} %get-tuple-element.20), channel_id=1, replica_groups=mesh['probe'=4,'space'=8] {'probe','space'}, use_global_device_ids=true, to_apply=%region_17.18 | all-reduce | flops 1 | bytes 8 | tf_op jit(solution)/shard_map/psum | solution.py:64
  155.4 3.5 %copy.7 = f32[48,8,1024]{2,1,0:T(8,128)} copy(f32[48,8,1024]{2,0,1:T(8,128)} %get-tuple-element.21) | data formatting | bytes 3145728
  (48 shorter events, 8.0 us)
Async XLA Ops:
  0.6 6.3 %copy-start.6 = (f32[8,1024]{1,0:T(8,128)S(1)}, f32[8,1024]{1,0:T(8,128)}, u32[]{:S(2)}) copy-start(f32[8,1024]{1,0:T(8,128)} %param.7) | copy-start | bytes 98308
  0.6 6.3 %copy-start.7 = (f32[8,1024]{1,0:T(8,128)S(1)}, f32[8,1024]{1,0:T(8,128)}, u32[]{:S(2)}) copy-start(f32[8,1024]{1,0:T(8,128)} %param.6) | copy-start | bytes 98308
  0.7 6.3 %copy-start.8 = (s32[8,1024]{1,0:T(8,128)S(1)}, s32[8,1024]{1,0:T(8,128)}, u32[]{:S(2)}) copy-start(s32[8,1024]{1,0:T(8,128)} %param.5) | copy-start | bytes 98308
  3.2 3.8 %collective-permute-start.1 = (f32[48,1,1024]{2,0,1:T(8,128)S(1)}, f32[48,1,1024]{2,0,1:T(8,128)S(1)}, u32[]{:S(2)}, u32[]{:S(2)}) collective-permute-start(f32[48,1,1024]{2,0,1:T(8,128)S(1)} %get-tuple-element.38), channel_id=1, source_target_pairs={{0,1},{1,2},{2,3},{3,4},{4,5},{5,6},{6,7},{8,9},{9,10},{10,11},{11... | collective-permute-start | bytes 589832 | tf_op jit(solution)/shard_map/ppermute | solution.py:17
  5.6 5.5 %collective-permute-start = (f32[48,1,1024]{2,0,1:T(8,128)S(1)}, f32[48,1,1024]{2,0,1:T(8,128)S(1)}, u32[]{:S(2)}, u32[]{:S(2)}) collective-permute-start(f32[48,1,1024]{2,0,1:T(8,128)S(1)} %get-tuple-element.39), channel_id=1, source_target_pairs={{1,0},{2,1},{3,2},{4,3},{5,4},{6,5},{7,6},{9,8},{10,9},{11,10},{12... | collective-permute-start | bytes 589832 | tf_op jit(solution)/shard_map/ppermute | solution.py:19
  7.0 33.3 %copy-start.3 = (f32[8,1024]{1,0:T(8,128)}, f32[8,1024]{1,0:T(8,128)S(1)}, u32[]{:S(2)}) copy-start(f32[8,1024]{1,0:T(8,128)S(1)} %add_add_fusion) | copy-start | bytes 98308
  7.0 4.8 %copy-start.2 = (s32[48,8,1024]{2,1,0:T(8,128)S(1)}, s32[48,8,1024]{2,1,0:T(8,128)}, u32[]{:S(2)}) copy-start(s32[48,8,1024]{2,1,0:T(8,128)} %param.4) | copy-start | bytes 4718596
  32.3 2.6 %copy-start.9 = (f32[48]{0:T(128)}, f32[48]{0:T(128)S(1)}, u32[]{:S(2)}) copy-start(f32[48]{0:T(128)S(1)} %div.33) | copy-start | bytes 580
  35.0 2.6 %collective-permute-start.3 = (f32[48,1,1024]{2,0,1:T(8,128)S(1)}, f32[48,1,1024]{2,0,1:T(8,128)S(1)}, u32[]{:S(2)}, u32[]{:S(2)}) collective-permute-start(f32[48,1,1024]{2,0,1:T(8,128)S(1)} %get-tuple-element.36), channel_id=1, source_target_pairs={{0,1},{1,2},{2,3},{3,4},{4,5},{5,6},{6,7},{8,9},{9,10},{10,11},{11... | collective-permute-start | bytes 589832 | tf_op jit(solution)/shard_map/ppermute | solution.py:17
  36.3 3.3 %collective-permute-start.2 = (f32[48,1,1024]{2,0,1:T(8,128)S(1)}, f32[48,1,1024]{2,0,1:T(8,128)S(1)}, u32[]{:S(2)}, u32[]{:S(2)}) collective-permute-start(f32[48,1,1024]{2,0,1:T(8,128)S(1)} %get-tuple-element.37), channel_id=1, source_target_pairs={{1,0},{2,1},{3,2},{4,3},{5,4},{6,5},{7,6},{9,8},{10,9},{11,10},{12... | collective-permute-start | bytes 589832 | tf_op jit(solution)/shard_map/ppermute | solution.py:19
  58.5 0.5 copy-start.11
  61.5 2.6 %collective-permute-start.5 = (f32[48,1,1024]{2,0,1:T(8,128)S(1)}, f32[48,1,1024]{2,0,1:T(8,128)S(1)}, u32[]{:S(2)}, u32[]{:S(2)}) collective-permute-start(f32[48,1,1024]{2,0,1:T(8,128)S(1)} %get-tuple-element.34), channel_id=1, source_target_pairs={{0,1},{1,2},{2,3},{3,4},{4,5},{5,6},{6,7},{8,9},{9,10},{10,11},{11... | collective-permute-start | bytes 589832 | tf_op jit(solution)/shard_map/ppermute | solution.py:17
  62.8 4.0 %copy-start.4 = (f32[8,1024]{1,0:T(8,128)S(1)}, f32[8,1024]{1,0:T(8,128)}, u32[]{:S(2)}) copy-start(f32[8,1024]{1,0:T(8,128)} %copy-done.3) | copy-start | bytes 98308
  62.8 3.3 %collective-permute-start.4 = (f32[48,1,1024]{2,0,1:T(8,128)S(1)}, f32[48,1,1024]{2,0,1:T(8,128)S(1)}, u32[]{:S(2)}, u32[]{:S(2)}) collective-permute-start(f32[48,1,1024]{2,0,1:T(8,128)S(1)} %get-tuple-element.35), channel_id=1, source_target_pairs={{1,0},{2,1},{3,2},{4,3},{5,4},{6,5},{7,6},{9,8},{10,9},{11,10},{12... | collective-permute-start | bytes 589832 | tf_op jit(solution)/shard_map/ppermute | solution.py:19
  66.8 1.4 copy-start
  89.9 5.3 %copy-start.1 = (f32[48,8,1024]{2,0,1:T(8,128)}, f32[48,8,1024]{2,0,1:T(8,128)S(1)}, u32[]{:S(2)}) copy-start(f32[48,8,1024]{2,0,1:T(8,128)S(1)} %multiply_subtract_fusion) | copy-start | bytes 4718596
  90.0 2.6 %collective-permute-start.7 = (f32[48,1,1024]{2,0,1:T(8,128)S(1)}, f32[48,1,1024]{2,0,1:T(8,128)S(1)}, u32[]{:S(2)}, u32[]{:S(2)}) collective-permute-start(f32[48,1,1024]{2,0,1:T(8,128)S(1)} %get-tuple-element.32), channel_id=1, source_target_pairs={{0,1},{1,2},{2,3},{3,4},{4,5},{5,6},{6,7},{8,9},{9,10},{10,11},{11... | collective-permute-start | bytes 589832 | tf_op jit(solution)/shard_map/ppermute | solution.py:17
  91.3 4.0 %copy-start.5 = (f32[8,1024]{1,0:T(8,128)S(1)}, f32[8,1024]{1,0:T(8,128)}, u32[]{:S(2)}) copy-start(f32[8,1024]{1,0:T(8,128)} %copy-done.3) | copy-start | bytes 98308
  91.3 3.3 %collective-permute-start.6 = (f32[48,1,1024]{2,0,1:T(8,128)S(1)}, f32[48,1,1024]{2,0,1:T(8,128)S(1)}, u32[]{:S(2)}, u32[]{:S(2)}) collective-permute-start(f32[48,1,1024]{2,0,1:T(8,128)S(1)} %get-tuple-element.33), channel_id=1, source_target_pairs={{1,0},{2,1},{3,2},{4,3},{5,4},{6,5},{7,6},{9,8},{10,9},{11,10},{12... | collective-permute-start | bytes 589832 | tf_op jit(solution)/shard_map/ppermute | solution.py:19
  95.3 17.0 %copy-start.12 = (f32[48]{0:T(128)S(1)}, f32[48]{0:T(128)}, u32[]{:S(2)}) copy-start(f32[48]{0:T(128)} %get-tuple-element.14) | copy-start | bytes 580
  95.3 17.0 %copy-start.13 = (f32[48]{0:T(128)S(1)}, f32[48]{0:T(128)}, u32[]{:S(2)}) copy-start(f32[48]{0:T(128)} %get-tuple-element.25) | copy-start | bytes 580
  95.3 17.0 %copy-start.10 = (f32[48]{0:T(128)S(1)}, f32[48]{0:T(128)}, u32[]{:S(2)}) copy-start(f32[48]{0:T(128)} %copy-done.9) | copy-start | bytes 580
where the time goes:
time: 162 us; the launch traced here: 161 us
  blocking collectives  105 us (65%)
  other arithmetic  27.3 us (17%)
  starting transfers between devices  11.5 us (7%)
  waiting for transfers between devices  10.2 us (6%)
  local copies, waits for them, and re-layouts  4.18 us (3%)
  between operations  2.76 us (2%)
    psum x4, blocking collectives, two_sums(): lax.psum((per_probe(residual * residual), per_probe(residual * applied)),...  66.7 us
    psum x1, blocking collectives, on_device(): trace_sum = lax.psum(local_part, ('probe', 'space'))  38 us
    ppermute x4, waiting for transfers between devices, with_halo(): lax.ppermute(head, axis, [((i + 1) % count, i) for i in range(ends)])  10.2 us
    sub x3, other arithmetic, on_device(): residual = residual - step_len[:, None, None] * applied_dir  8.99 us
    reduce_sum x4, other arithmetic, per_probe(): return jnp.sum(values, axis=(1, 2))  6.44 us
    ppermute x4, starting transfers between devices, with_halo(): lax.ppermute(tail, axis, [(i, (i + 1) % count) for i in range(ends)])  6.31 us
    ppermute x4, starting transfers between devices, with_halo(): lax.ppermute(head, axis, [((i + 1) % count, i) for i in range(ends)])  5.17 us
    reduce_sum x1, other arithmetic, on_device(): local_part = jnp.sum(probes * solution)  5.06 us
  transfers between devices with their start and end apart: 8, of which 4 were waited for; matrix products, arithmetic and copies ran while one was open for 0% of the time, Pallas kernels for 0%

commit v1 on v0

v1 whole, which is shorter than its diff:
```python
import functools

import jax
import jax.numpy as jnp
from jax import lax
from jax.experimental import pallas as pl
from jax.experimental.pallas import tpu as pltpu
from jax.sharding import PartitionSpec as P

MESH = pl.DeviceIdType.MESH
LANES = 128
SHIFT = 4.0
LOW = 0.02
TINY = 1e-30


def split(block):
    return [block[:, t * LANES : (t + 1) * LANES] for t in range(block.shape[1] // LANES)]


def sideways(tiles, lane):
    ahead = [pltpu.roll(v, 1, 1) for v in tiles]
    behind = [pltpu.roll(v, LANES - 1, 1) for v in tiles]
    zero = jnp.zeros_like(tiles[0])
    count = len(tiles)
    out = []
    for t in range(count):
        west = jnp.where(lane == 0, ahead[t - 1] if t else zero, ahead[t])
        east = jnp.where(lane == LANES - 1, behind[t + 1] if t + 1 < count else zero, behind[t])
        out.append(west + east)
    return out


def upright(own, halo, row, want_own, want_halo):
    rows = own[0].shape[0]
    for_own, for_halo = [], []
    for o, h in zip(own, halo):
        o_down, h_down = pltpu.roll(o, 1, 0), pltpu.roll(h, 1, 0)
        o_up, h_up = pltpu.roll(o, rows - 1, 0), pltpu.roll(h, rows - 1, 0)
        if want_own:
            for_own.append(jnp.where(row == 0, h_down, o_down) + jnp.where(row == rows - 1, h_up, o_up))
        if want_halo:
            for_halo.append(jnp.where(row == 0, o_down, h_down) + jnp.where(row == rows - 1, o_up, h_up))
    return for_own, for_halo


def apply_own(own, halo, diag, lane, row):
    up, _ = upright(own, halo, row, True, False)
    side = sideways(own, lane)
    return [d * v - (u + s) for d, v, u, s in zip(diag, own, up, side)]


def apply_halo(own, halo, diag, mask, lane, row):
    _, up = upright(own, halo, row, False, True)
    side = sideways(halo, lane)
    return [d * v - mask * (u + s) for d, v, u, s in zip(diag, halo, up, side)]


def apply_both(own, halo, diag, diag_h, mask, lane, row):
    up, up_h = upright(own, halo, row, True, True)
    side, side_h = sideways(own, lane), sideways(halo, lane)
    return (
        [d * v - (u + s) for d, v, u, s in zip(diag, own, up, side)],
        [d * v - mask * (u + s) for d, v, u, s in zip(diag_h, halo, up_h, side_h)],
    )


def dot(left, right):
    total = left[0] * right[0]
    for a, b in zip(left[1:], right[1:]):
        total = total + a * b
    return jnp.sum(total, axis=0, keepdims=True)


def first_steps(m1, m2, m3, m4):
    sigma = SHIFT
    a0 = sigma + m1
    b1 = jnp.maximum(m2 - m1 * m1, 0.0)
    h3 = m3 - 2.0 * m1 * m2 + m1 * m1 * m1
    s0 = 1.0 / jnp.maximum(a0, LOW)
    rr1 = s0 * s0 * b1
    pq1 = s0 * s0 * (h3 + sigma * b1) - rr1 * rr1 / s0
    s1 = rr1 / jnp.maximum(jnp.maximum(pq1, LOW * rr1), TINY)
    p1b, p1g = s0 * m1 + rr1, -s0
    r2b = s0 * m1 - s1 * sigma * p1b
    r2g = -s0 - s1 * (sigma * p1g + p1b)
    r2y = -s1 * p1g
    rr2 = jnp.maximum(r2y * (r2b * m2 + r2g * m3 + r2y * m4), 0.0)
    be1 = rr2 / jnp.maximum(rr1, TINY)
    p2b, p2g, p2y = r2b + be1 * p1b, r2g + be1 * p1g, r2y
    return dict(s0=s0, s1=s1, p1b=p1b, p1g=p1g, pq1=pq1, be1=be1, r2=(r2b, r2g, r2y), p2=(p2b, p2g, p2y))


def last_steps(st, sums):
    rr, rp, pp, pq, rq, qq, rw, qw = sums
    sigma = SHIFT
    full_pq = pq + sigma * pp
    s2 = rr / jnp.maximum(jnp.maximum(full_pq, LOW * rr), TINY)
    full_rq = rq + sigma * rp
    full_qq = qq + 2.0 * sigma * pq + sigma * sigma * pp
    rr3 = jnp.maximum(rr - 2.0 * s2 * full_rq + s2 * s2 * full_qq, 0.0)
    be2 = rr3 / jnp.maximum(rr, TINY)
    rhr2 = full_pq + st["be1"] * st["be1"] * st["pq1"]
    rhq = rw + 2.0 * sigma * rq + sigma * sigma * rp
    qhq = qw + 3.0 * sigma * qq + 3.0 * sigma * sigma * pq + sigma * sigma * sigma * pp
    rhr3 = rhr2 - 2.0 * s2 * rhq + s2 * s2 * qhq
    pq3 = rhr3 - rr3 * rr3 / jnp.maximum(rr * s2, TINY)
    s3 = rr3 / jnp.maximum(jnp.maximum(pq3, LOW * rr3), TINY)
    cp, cr, cq = s2 + s3 * (be2 - s2 * sigma), s3, -s3 * s2
    r2, p2 = st["r2"], st["p2"]
    xb = st["s0"] + st["s1"] * st["p1b"] + cp * p2[0] + cr * r2[0]
    xg = st["s1"] * st["p1g"] + cp * p2[1] + cr * r2[1]
    xy = cp * p2[2] + cr * r2[2]
    return xb, xg, xy, cq


def kernel(
    names, chunk, signs_hbm, mask_ref, weight_ref, prior_ref, out_hbm, trace_ref,
    signs, halo, halo_far, diag, diag_h, g_own, g_halo, y_own, y_halo, q_own, x_own,
    acc, mine, parts, tr_mine, tr_parts, coef,
    load_sem, out_sem, dsend, drecv, hsend, hrecv, ssend, srecv, tsend, trecv,
):
    probe_axis, space_axis = names
    probe, space = lax.axis_index(probe_axis), lax.axis_index(space_axis)
    probe_n, space_n = lax.axis_size(probe_axis), lax.axis_size(space_axis)
    probes, rows, cols = signs.shape
    half = rows // 2
    quarter = half // 2
    chunks = probes // chunk
    cells = float(rows * space_n * cols)

    barrier = pltpu.get_barrier_semaphore()
    for k in range(1, space_n):
        pl.semaphore_signal(barrier, 1, device_id=(probe, lax.rem(space + k, space_n)), device_id_type=MESH)
    for k in range(1, probe_n):
        pl.semaphore_signal(barrier, 1, device_id=(lax.rem(probe + k, probe_n), space), device_id_type=MESH)
    loads = pltpu.make_async_copy(signs_hbm, signs, load_sem)
    loads.start()
    diag[...] = mask_ref[...].astype(jnp.float32) * weight_ref[...] + prior_ref[...]
    loads.wait()
    pl.semaphore_wait(barrier, space_n + probe_n - 2)

    has_prev, has_next = space > 0, space < space_n - 1
    prev, nxt = (probe, jnp.maximum(space - 1, 0)), (probe, jnp.minimum(space + 1, space_n - 1))

    def pieces(stage):
        if stage == 0:
            return (0, quarter), (rows - quarter, quarter)
        return (quarter, half - quarter), (half, half - quarter)

    def halo_copy(stage, c, side):
        start, size = pieces(stage)[side]
        at = (pl.ds(c * chunk, chunk), pl.ds(start, size))
        return pltpu.make_async_remote_copy(
            src_ref=signs.at[at], dst_ref=(halo, halo_far)[stage].at[at],
            send_sem=hsend.at[stage, side, c], recv_sem=hrecv.at[stage, side, c],
            device_id=(prev, nxt)[side], device_id_type=MESH,
        )

    def diag_copy(side):
        at = pl.ds(side * half, half)
        return pltpu.make_async_remote_copy(
            src_ref=diag.at[at], dst_ref=diag_h.at[at],
            send_sem=dsend.at[side], recv_sem=drecv.at[side],
            device_id=(prev, nxt)[side], device_id_type=MESH,
        )

    for side, there in ((0, has_prev), (1, has_next)):
        @pl.when(there)
        def _():
            diag_copy(side).start()
    for stage in (0, 1):
        for c in range(chunks):
            for side, there in ((0, has_prev), (1, has_next)):
                @pl.when(there)
                def _():
                    halo_copy(stage, c, side).start()

    for side, there in ((0, has_next), (1, has_prev)):
        @pl.when(there)
        def _():
            diag_copy(side).wait_recv()

    row = lax.broadcasted_iota(jnp.int32, (rows, LANES), 0)
    lane = lax.broadcasted_iota(jnp.int32, (rows, LANES), 1)
    below = jnp.where(has_next, 1.0, 0.0)
    above = jnp.where(has_prev, 1.0, 0.0)
    mask = jnp.where(row < half, below, above)
    live = mask > 0.5
    wide = lax.broadcasted_iota(jnp.int32, (rows, cols), 0)
    diag_h[...] = jnp.where(jnp.where(wide < half, below, above) > 0.5, diag_h[...], 0.0)

    def field(ref, p):
        return split(2.0 * ref[p].astype(jnp.float32) - 1.0)

    near = (row < quarter) | (row >= rows - quarter)

    def near_field(p):
        return [jnp.where(live & near, v, 0.0) for v in field(halo, p)]

    def halo_field(p):
        pairs = zip(split(halo[p]), split(halo_far[p]))
        return [jnp.where(live, 2.0 * jnp.where(near, a, b).astype(jnp.float32) - 1.0, 0.0) for a, b in pairs]

    def keep(ref, p, tiles):
        for t, v in enumerate(tiles):
            ref[p, :, t * LANES : (t + 1) * LANES] = v

    def first(p, carry):
        own, out = field(signs, p), near_field(p)
        d, dh = split(diag[...]), split(diag_h[...])
        g, gh = apply_both(own, out, d, dh, mask, lane, row)
        y = apply_own(g, gh, d, lane, row)
        keep(g_own, p, g)
        keep(y_own, p, y)
        for k, (a, b) in enumerate(((own, g), (g, g), (g, y), (y, y))):
            acc[k, pl.ds(p, 1), :] = dot(a, b)
        return carry

    def second(p, carry):
        own, out = field(signs, p), halo_field(p)
        dh = split(diag_h[...])
        g = split(g_own[p])
        gh = apply_halo(own, out, dh, mask, lane, row)
        yh = apply_halo(g, gh, dh, mask, lane, row)
        keep(g_halo, p, gh)
        keep(y_halo, p, yh)
        return carry

    def await_halo(stage, c):
        for side, there in ((0, has_next), (1, has_prev)):
            @pl.when(there)
            def _():
                halo_copy(stage, c, side).wait_recv()

    for c in range(chunks):
        await_halo(0, c)
        lax.fori_loop(c * chunk, (c + 1) * chunk, first, 0)

    def sum_copy(which, k):
        other = lax.rem(space + k, space_n)
        return pltpu.make_async_remote_copy(
            src_ref=mine.at[which], dst_ref=parts.at[which, k],
            send_sem=ssend.at[which, k], recv_sem=srecv.at[which, k],
            device_id=(probe, other), device_id_type=MESH,
        )

    def send_sums(which, count):
        wide_lane = lax.broadcasted_iota(jnp.int32, (probes, LANES), 1)
        table = jnp.zeros((probes, LANES), jnp.float32)
        for k in range(count):
            table = jnp.where(wide_lane == k, jnp.sum(acc[k], axis=1, keepdims=True), table)
        table = jnp.concatenate([table, jnp.zeros((LANES - probes, LANES), jnp.float32)], axis=0)
        mine[which] = jnp.transpose(table)[:8]
        for k in range(1, space_n):
            sum_copy(which, k).start()

    def take_sums(which):
        for k in range(1, space_n):
            sum_copy(which, k).wait_recv()
        parts[which, 0] = mine[which]
        total = None
        for s in range(space_n):
            part = parts[which, lax.rem(space - s + space_n, space_n)]
            total = part if total is None else total + part
        total = total / cells
        return [total[k : k + 1] for k in range(8)]

    def spread(values):
        r8 = lax.broadcasted_iota(jnp.int32, (8, LANES), 0)
        table = jnp.zeros((8, LANES), jnp.float32)
        for k, v in enumerate(values):
            table = jnp.where(r8 == k, jnp.broadcast_to(v, (8, LANES)), table)
        table = jnp.concatenate([table, jnp.zeros((LANES - 8, LANES), jnp.float32)], axis=0)
        columns = jnp.transpose(table)
        for k in range(len(values)):
            coef[k] = jnp.broadcast_to(columns[:probes, k : k + 1], (probes, LANES))

    def combine(scales, *fields):
        out = []
        for tiles in zip(*fields):
            total = scales[0] * tiles[0]
            for s, v in zip(scales[1:], tiles[1:]):
                total = total + s * v
            out.append(total)
        return out

    def scale(k, p):
        return jnp.broadcast_to(coef[k, pl.ds(p, 1), :], (rows, LANES))

    send_sums(0, 4)
    for c in range(chunks):
        await_halo(1, c)
        lax.fori_loop(c * chunk, (c + 1) * chunk, second, 0)
    m1, m2, m3, m4 = take_sums(0)[:4]
    st = first_steps(m1, m2, m3, m4)
    spread(st["r2"] + st["p2"])

    def third(p, carry):
        own, out = field(signs, p), halo_field(p)
        g, y = split(g_own[p]), split(y_own[p])
        d, dh = split(diag[...]), split(diag_h[...])
        cs = [scale(k, p) for k in range(6)]
        p2 = combine(cs[3:], own, g, y)
        p2h = combine(cs[3:], out, split(g_halo[p]), split(y_halo[p]))
        q, qh = apply_both(p2, p2h, d, dh, mask, lane, row)
        keep(q_own, p, q)
        w = apply_own(q, qh, d, lane, row)
        r2 = combine(cs[:3], own, g, y)
        pairs = ((r2, r2), (r2, p2), (p2, p2), (p2, q), (r2, q), (q, q), (r2, w), (q, w))
        for k, (a, b) in enumerate(pairs):
            acc[k, pl.ds(p, 1), :] = dot(a, b)
        return carry

    lax.fori_loop(0, probes, third, 0)
    send_sums(1, 8)
    xb, xg, xy, cq = last_steps(st, take_sums(1))
    p2 = st["p2"]
    trace = xb + xg * m1 + xy * m2 + cq * (p2[0] * m1 + p2[1] * m2 + p2[2] * m3)
    lane1 = lax.broadcasted_iota(jnp.int32, (1, LANES), 1)
    trace = jnp.where(lane1 < probes, trace, 0.0)
    tr_mine[...] = jnp.broadcast_to(trace, tr_mine.shape)

    def trace_copy(k):
        return pltpu.make_async_remote_copy(
            src_ref=tr_mine, dst_ref=tr_parts.at[k],
            send_sem=tsend.at[k], recv_sem=trecv.at[k],
            device_id=(lax.rem(probe + k, probe_n), space), device_id_type=MESH,
        )

    spread((xb, xg, xy, cq))
    for k in range(1, probe_n):
        trace_copy(k).start()

    def fourth(p, carry):
        x = combine([scale(k, p) for k in range(4)], field(signs, p), split(g_own[p]), split(y_own[p]), split(q_own[p]))
        keep(x_own, p, x)
        return carry

    def out_copy(c):
        at = pl.ds(c * chunk, chunk)
        return pltpu.make_async_copy(x_own.at[at], out_hbm.at[at], out_sem.at[c])

    for c in range(chunks):
        lax.fori_loop(c * chunk, (c + 1) * chunk, fourth, 0)
        out_copy(c).start()

    for k in range(1, probe_n):
        trace_copy(k).wait_recv()
    tr_parts[0] = tr_mine[...]
    total = None
    for s in range(probe_n):
        part = tr_parts[lax.rem(probe - s + probe_n, probe_n)]
        total = part if total is None else total + part
    trace_ref[0, 0] = jnp.sum(total[0:1]) * (1.0 / float(probes * probe_n))

    for side, there in ((0, has_prev), (1, has_next)):
        @pl.when(there)
        def _():
            diag_copy(side).wait_send()
            for stage in (0, 1):
                for c in range(chunks):
                    halo_copy(stage, c, side).wait_send()
    for which in (0, 1):
        for k in range(1, space_n):
            sum_copy(which, k).wait_send()
    for k in range(1, probe_n):
        trace_copy(k).wait_send()
    for c in range(chunks):
        out_copy(c).wait()


def solution(mesh):
    probe_n, space_n = mesh.shape["probe"], mesh.shape["space"]

    def on_device(probe_signs, sensor_mask, sensor_weight, prior_mass):
        probes, rows, cols = probe_signs.shape
        chunk = next(c for c in (8, 6, 4, 3, 2, 1) if probes % c == 0)
        chunks = probes // chunk
        full = (probes, rows, cols)
        dma = pltpu.SemaphoreType.DMA
        vmem = pl.BlockSpec(memory_space=pltpu.VMEM)
        f32 = jnp.float32
        solved, trace = pl.pallas_call(
            functools.partial(kernel, ("probe", "space"), chunk),
            out_shape=(jax.ShapeDtypeStruct(full, f32), jax.ShapeDtypeStruct((1, 1), f32)),
            in_specs=[pl.BlockSpec(memory_space=pl.ANY), vmem, vmem, vmem],
            out_specs=(pl.BlockSpec(memory_space=pl.ANY), pl.BlockSpec(memory_space=pltpu.SMEM)),
            scratch_shapes=[
                pltpu.VMEM(full, jnp.int32), pltpu.VMEM(full, jnp.int32), pltpu.VMEM(full, jnp.int32),
                pltpu.VMEM((rows, cols), f32), pltpu.VMEM((rows, cols), f32),
                pltpu.VMEM(full, f32), pltpu.VMEM(full, f32), pltpu.VMEM(full, f32), pltpu.VMEM(full, f32),
                pltpu.VMEM(full, f32), pltpu.VMEM(full, f32),
                pltpu.VMEM((8, probes, LANES), f32),
                pltpu.VMEM((2, 8, LANES), f32), pltpu.VMEM((2, space_n, 8, LANES), f32),
                pltpu.VMEM((8, LANES), f32), pltpu.VMEM((probe_n, 8, LANES), f32),
                pltpu.VMEM((8, probes, LANES), f32),
                dma, dma((chunks,)), dma((2,)), dma((2,)),
                dma((2, 2, chunks)), dma((2, 2, chunks)),
                dma((2, space_n)), dma((2, space_n)), dma((probe_n,)), dma((probe_n,)),
            ],
            compiler_params=pltpu.CompilerParams(collective_id=0, has_side_effects=True),
            name="cg",
        )(probe_signs, sensor_mask, sensor_weight, prior_mass)
        return solved, trace.reshape(())

    return jax.shard_map(
        on_device,
        mesh=mesh,
        in_specs=(P("probe", "space", None), P("space", None), P("space", None), P("space", None)),
        out_specs=(P("probe", "space", None), P()),
        check_vma=False,
    )
```

time: 162 us -> 49 us (0.30)
  blocking collectives: 105 us -> 0 us
  Pallas kernels: 0 us -> 43.6 us
  other arithmetic: 27.3 us -> 0 us
  starting transfers between devices: 11.5 us -> 0 us
  waiting for transfers between devices: 10.2 us -> 0 us
    psum x5 -> x0, blocking collectives: 105 us -> none  [the longest x4 66.7 us: two_sums(): lax.psum((per_probe(residual * residual), per_probe(residual * applied)),...]
    pallas_call x0 -> x1, Pallas kernels: none -> 43.6 us  [on_device(): pl.pallas_call(functools.partial(kernel, ('probe', 'space'), chunk), out_...]
    sub x4 -> x0, other arithmetic: 11.5 us -> none  [the longest x3 8.99 us: on_device(): residual = residual - step_len[:, None, None] * applied_dir]
    reduce_sum x5 -> x0, other arithmetic: 11.5 us -> none  [the longest x4 6.44 us: per_probe(): return jnp.sum(values, axis=(1, 2))]
    ppermute x8 -> x0, starting transfers between devices: 11.5 us -> none  [the longest x4 6.31 us: with_halo(): lax.ppermute(tail, axis, [(i, (i + 1) % count) for i in range(ends)])]
    ppermute x8 -> x0, waiting for transfers between devices: 10.2 us -> none  [the longest x4 10.2 us: with_halo(): lax.ppermute(head, axis, [((i + 1) % count, i) for i in range(ends)])]
    concatenate x4 -> x0, other arithmetic: 2.54 us -> none  [with_halo(): jnp.concatenate([lax.ppermute(tail, axis, [(i, (i + 1) % count) for i in...]
    div x4 -> x0, other arithmetic: 1.75 us -> none  [the longest x3 1.75 us: on_device(): step_len = norm_next / (curvature - step_ratio * norm_next / step_len)]
  transfers between devices with their start and end apart: 8 -> 0, of which waited for: 4 -> 0; matrix products, arithmetic and copies ran while one was open for 0% -> 0% of each run, Pallas kernels for 0% -> 0%
where the time goes in v1:
time: 49 us; the launch traced here: 48.7 us
  Pallas kernels  43.6 us (89%)
  local copies, waits for them, and re-layouts  2.73 us (6%)
  between operations  2.41 us (5%)
    pallas_call x1, Pallas kernels, on_device(): pl.pallas_call(functools.partial(kernel, ('probe', 'space'), chunk), out_...  43.6 us
    unnamed x1, local copies, waits for them, and re-layouts  2.73 us

profile of v1, /device:TPU:0, one launch (start us, length us, event | category | flops | bytes accessed | tf_op | source)
XLA Modules:
  0.0 48.7 jit_solution(13175484616333979955)
XLA Ops:
  0.6 43.6 %cg.1 = (f32[48,8,1024]{2,1,0:T(8,128)}, f32[1,1]{1,0:T(1,128)}) custom-call(s32[48,8,1024]{2,1,0:T(8,128)} %signs_hbm.1, s32[8,1024]{1,0:T(8,128)} %mask_ref.1, f32[8,1024]{1,0:T(8,128)} %weight_ref.1, f32[8,1024]{1,0:T(8,128)} %prior_ref.1), custom_call_target="tpu_custom_call" | custom-call | tf_op jit(solution)/shard_map/cg/pallas_call | solution.py:384
  44.2 2.7 %copy.8 = f32[48,8,1024]{2,1,0:T(8,128)} copy(f32[48,8,1024]{2,1,0:T(8,128)} %get-tuple-element.8) | data formatting | bytes 3145728

commit v2 on v1

--- a/solution.py
+++ b/solution.py
@@ -115,10 +115,10 @@
 
 
 def kernel(
-    names, chunk, signs_hbm, mask_ref, weight_ref, prior_ref, out_hbm, trace_ref,
-    signs, halo, halo_far, diag, diag_h, g_own, g_halo, y_own, y_halo, q_own, x_own,
+    names, chunk, signs_hbm, mask_ref, weight_ref, prior_ref, x_own, trace_ref,
+    signs, halo, halo_far, b_own, b_halo, diag, diag_h, g_own, g_halo, y_own, y_halo, q_own,
     acc, mine, parts, tr_mine, tr_parts, coef,
-    load_sem, out_sem, dsend, drecv, hsend, hrecv, ssend, srecv, tsend, trecv,
+    load_sem, dsend, drecv, hsend, hrecv, ssend, srecv, tsend, trecv, space_in, probe_in,
 ):
     probe_axis, space_axis = names
     probe, space = lax.axis_index(probe_axis), lax.axis_index(space_axis)
@@ -130,18 +130,35 @@
     cells = float(rows * space_n * cols)
 
     barrier = pltpu.get_barrier_semaphore()
-    for k in range(1, space_n):
-        pl.semaphore_signal(barrier, 1, device_id=(probe, lax.rem(space + k, space_n)), device_id_type=MESH)
-    for k in range(1, probe_n):
-        pl.semaphore_signal(barrier, 1, device_id=(lax.rem(probe + k, probe_n), space), device_id_type=MESH)
+    has_prev, has_next = space > 0, space < space_n - 1
+    prev, nxt = (probe, jnp.maximum(space - 1, 0)), (probe, jnp.minimum(space + 1, space_n - 1))
+
+    def meet(sem, distance):
+        for there, other in (
+            (space >= distance, jnp.maximum(space - distance, 0)),
+            (space + distance < space_n, jnp.minimum(space + distance, space_n - 1)),
+        ):
+            @pl.when(there)
+            def _():
+                pl.semaphore_signal(sem, 1, device_id=(probe, other), device_id_type=MESH)
+
+    def met(distance):
+        return jnp.where(space >= distance, 1, 0) + jnp.where(space + distance < space_n, 1, 0)
+
+    def flip(bit):
+        size = 1 << bit
+        return probe + size * (1 - 2 * lax.rem(probe // size, 2))
+
+    probe_bits = (probe_n - 1).bit_length()
+    space_bits = (space_n - 1).bit_length()
+    meet(barrier, 1)
+    for bit in range(probe_bits):
+        pl.semaphore_signal(barrier, 1, device_id=(flip(bit), space), device_id_type=MESH)
     loads = pltpu.make_async_copy(signs_hbm, signs, load_sem)
     loads.start()
     diag[...] = mask_ref[...].astype(jnp.float32) * weight_ref[...] + prior_ref[...]
     loads.wait()
-    pl.semaphore_wait(barrier, space_n + probe_n - 2)
-
-    has_prev, has_next = space > 0, space < space_n - 1
-    prev, nxt = (probe, jnp.maximum(space - 1, 0)), (probe, jnp.minimum(space + 1, space_n - 1))
+    pl.semaphore_wait(barrier, met(1) + probe_bits)
 
     def pieces(stage):
         if stage == 0:
@@ -211,6 +228,7 @@
         d, dh = split(diag[...]), split(diag_h[...])
         g, gh = apply_both(own, out, d, dh, mask, lane, row)
         y = apply_own(g, gh, d, lane, row)
+        keep(b_own, p, own)
         keep(g_own, p, g)
         keep(y_own, p, y)
         for k, (a, b) in enumerate(((own, g), (g, g), (g, y), (y, y))):
@@ -218,7 +236,8 @@
         return carry
 
     def second(p, carry):
-        own, out = field(signs, p), halo_field(p)
+        own, out = split(b_own[p]), halo_field(p)
+        keep(b_halo, p, out)
         dh = split(diag_h[...])
         g = split(g_own[p])
         gh = apply_halo(own, out, dh, mask, lane, row)
@@ -233,9 +252,27 @@
             def _():
                 halo_copy(stage, c, side).wait_recv()
 
-    for c in range(chunks):
-        await_halo(0, c)
-        lax.fori_loop(c * chunk, (c + 1) * chunk, first, 0)
+    def send_round(r):
+        meet(space_in.at[r], 1 << r)
+        for bit in range(probe_bits):
+            if r < probe_bits - 1:
+                pl.semaphore_signal(probe_in.at[r, bit], 1, device_id=(flip(bit), space), device_id_type=MESH)
+
+    def end_round(r):
+        pl.semaphore_wait(space_in.at[r], met(1 << r))
+        for bit in range(probe_bits):
+            if r < probe_bits - 1:
+                pl.semaphore_wait(probe_in.at[r, bit], 1)
+
+    rounds = max(space_bits, probe_bits - 1)
+    for c in range(max(chunks, rounds + 1)):
+        if 1 <= c <= rounds:
+            end_round(c - 1)
+        if c < rounds:
+            send_round(c)
+        if c < chunks:
+            await_halo(0, c)
+            lax.fori_loop(c * chunk, (c + 1) * chunk, first, 0)
 
     def sum_copy(which, k):
         other = lax.rem(space + k, space_n)
@@ -297,7 +334,7 @@
     spread(st["r2"] + st["p2"])
 
     def third(p, carry):
-        own, out = field(signs, p), halo_field(p)
+        own, out = split(b_own[p]), split(b_halo[p])
         g, y = split(g_own[p]), split(y_own[p])
         d, dh = split(diag[...]), split(diag_h[...])
         cs = [scale(k, p) for k in range(6)]
@@ -333,17 +370,11 @@
         trace_copy(k).start()
 
     def fourth(p, carry):
-        x = combine([scale(k, p) for k in range(4)], field(signs, p), split(g_own[p]), split(y_own[p]), split(q_own[p]))
+        x = combine([scale(k, p) for k in range(4)], split(b_own[p]), split(g_own[p]), split(y_own[p]), split(q_own[p]))
         keep(x_own, p, x)
         return carry
 
-    def out_copy(c):
-        at = pl.ds(c * chunk, chunk)
-        return pltpu.make_async_copy(x_own.at[at], out_hbm.at[at], out_sem.at[c])
-
-    for c in range(chunks):
-        lax.fori_loop(c * chunk, (c + 1) * chunk, fourth, 0)
-        out_copy(c).start()
+    lax.fori_loop(0, probes, fourth, 0)
 
     for k in range(1, probe_n):
         trace_copy(k).wait_recv()
@@ -366,8 +397,6 @@
             sum_copy(which, k).wait_send()
     for k in range(1, probe_n):
         trace_copy(k).wait_send()
-    for c in range(chunks):
-        out_copy(c).wait()
 
 
 def solution(mesh):
@@ -378,26 +407,28 @@
         chunk = next(c for c in (8, 6, 4, 3, 2, 1) if probes % c == 0)
         chunks = probes // chunk
         full = (probes, rows, cols)
-        dma = pltpu.SemaphoreType.DMA
+        dma, regular = pltpu.SemaphoreType.DMA, lambda n: pltpu.SemaphoreType.REGULAR(n)
         vmem = pl.BlockSpec(memory_space=pltpu.VMEM)
         f32 = jnp.float32
         solved, trace = pl.pallas_call(
             functools.partial(kernel, ("probe", "space"), chunk),
-            out_shape=(jax.ShapeDtypeStruct(full, f32), jax.ShapeDtypeStruct((1, 1), f32)),
+            out_shape=(pltpu.VMEM(full, f32), jax.ShapeDtypeStruct((1, 1), f32)),
             in_specs=[pl.BlockSpec(memory_space=pl.ANY), vmem, vmem, vmem],
-            out_specs=(pl.BlockSpec(memory_space=pl.ANY), pl.BlockSpec(memory_space=pltpu.SMEM)),
+            out_specs=(vmem, pl.BlockSpec(memory_space=pltpu.SMEM)),
             scratch_shapes=[
                 pltpu.VMEM(full, jnp.int32), pltpu.VMEM(full, jnp.int32), pltpu.VMEM(full, jnp.int32),
+                pltpu.VMEM(full, f32), pltpu.VMEM(full, f32),
                 pltpu.VMEM((rows, cols), f32), pltpu.VMEM((rows, cols), f32),
                 pltpu.VMEM(full, f32), pltpu.VMEM(full, f32), pltpu.VMEM(full, f32), pltpu.VMEM(full, f32),
-                pltpu.VMEM(full, f32), pltpu.VMEM(full, f32),
+                pltpu.VMEM(full, f32),
                 pltpu.VMEM((8, probes, LANES), f32),
                 pltpu.VMEM((2, 8, LANES), f32), pltpu.VMEM((2, space_n, 8, LANES), f32),
                 pltpu.VMEM((8, LANES), f32), pltpu.VMEM((probe_n, 8, LANES), f32),
                 pltpu.VMEM((8, probes, LANES), f32),
-                dma, dma((chunks,)), dma((2,)), dma((2,)),
+                dma, dma((2,)), dma((2,)),
                 dma((2, 2, chunks)), dma((2, 2, chunks)),
                 dma((2, space_n)), dma((2, space_n)), dma((probe_n,)), dma((probe_n,)),
+                regular((8,)), regular((8, 8)),
             ],
             compiler_params=pltpu.CompilerParams(collective_id=0, has_side_effects=True),
             name="cg",

time: 49 us -> 47.8 us (0.976)
  local copies, waits for them, and re-layouts: 2.73 us -> 1.15 us
  Pallas kernels: 43.6 us -> 44.1 us
    unnamed x1, local copies, waits for them, and re-layouts: 2.73 us -> 1.15 us
where the time goes in v2:
time: 47.8 us; the launch traced here: 47.5 us
  Pallas kernels  44.1 us (92%)
  between operations  2.33 us (5%)
  local copies, waits for them, and re-layouts  1.15 us (2%)
    pallas_call x1, Pallas kernels, on_device(): pl.pallas_call(functools.partial(kernel, ('probe', 'space'), chunk), out_...  44.1 us
    unnamed x1, local copies, waits for them, and re-layouts  1.15 us

profile of v2, /device:TPU:0, one launch (start us, length us, event | category | flops | bytes accessed | tf_op | source)
XLA Modules:
  0.0 47.5 jit_solution(5826939671532976019)
XLA Ops:
  0.6 44.1 %cg.1 = (f32[48,8,1024]{2,1,0:T(8,128)S(1)}, f32[1,1]{1,0:T(1,128)}) custom-call(s32[48,8,1024]{2,1,0:T(8,128)} %signs_hbm.1, s32[8,1024]{1,0:T(8,128)} %mask_ref.1, f32[8,1024]{1,0:T(8,128)} %weight_ref.1, f32[8,1024]{1,0:T(8,128)} %prior_ref.1), custom_call_target="tpu_custom_call" | custom-call | tf_op jit(solution)/shard_map/cg/pallas_call | solution.py:413
  44.7 1.1 %copy.8 = f32[48,8,1024]{2,1,0:T(8,128)} copy(f32[48,8,1024]{2,1,0:T(8,128)S(1)} %get-tuple-element.6) | data formatting | bytes 3145728

commit v3 on v2

--- a/solution.py
+++ b/solution.py
@@ -272,7 +272,7 @@
             send_round(c)
         if c < chunks:
             await_halo(0, c)
-            lax.fori_loop(c * chunk, (c + 1) * chunk, first, 0)
+            lax.fori_loop(c * chunk, (c + 1) * chunk, first, 0, unroll=4)
 
     def sum_copy(which, k):
         other = lax.rem(space + k, space_n)
@@ -328,7 +328,7 @@
     send_sums(0, 4)
     for c in range(chunks):
         await_halo(1, c)
-        lax.fori_loop(c * chunk, (c + 1) * chunk, second, 0)
+        lax.fori_loop(c * chunk, (c + 1) * chunk, second, 0, unroll=4)
     m1, m2, m3, m4 = take_sums(0)[:4]
     st = first_steps(m1, m2, m3, m4)
     spread(st["r2"] + st["p2"])
@@ -349,7 +349,7 @@
             acc[k, pl.ds(p, 1), :] = dot(a, b)
         return carry
 
-    lax.fori_loop(0, probes, third, 0)
+    lax.fori_loop(0, probes, third, 0, unroll=4)
     send_sums(1, 8)
     xb, xg, xy, cq = last_steps(st, take_sums(1))
     p2 = st["p2"]
@@ -365,16 +365,16 @@
             device_id=(lax.rem(probe + k, probe_n), space), device_id_type=MESH,
         )
 
-    spread((xb, xg, xy, cq))
     for k in range(1, probe_n):
         trace_copy(k).start()
+    spread((xb, xg, xy, cq))
 
     def fourth(p, carry):
         x = combine([scale(k, p) for k in range(4)], split(b_own[p]), split(g_own[p]), split(y_own[p]), split(q_own[p]))
         keep(x_own, p, x)
         return carry
 
-    lax.fori_loop(0, probes, fourth, 0)
+    lax.fori_loop(0, probes, fourth, 0, unroll=4)
 
     for k in range(1, probe_n):
         trace_copy(k).wait_recv()

time: 47.8 us -> 35.4 us (0.74)
  Pallas kernels: 44.1 us -> 31.7 us
    pallas_call x1, Pallas kernels: 44.1 us -> 31.7 us  [on_device(): pl.pallas_call(functools.partial(kernel, ('probe', 'space'), chunk), out_...]
where the time goes in v3:
time: 35.4 us; the launch traced here: 35.1 us
  Pallas kernels  31.7 us (90%)
  between operations  2.33 us (7%)
  local copies, waits for them, and re-layouts  1.15 us (3%)
    pallas_call x1, Pallas kernels, on_device(): pl.pallas_call(functools.partial(kernel, ('probe', 'space'), chunk), out_...  31.7 us
    unnamed x1, local copies, waits for them, and re-layouts  1.15 us

profile of v3, /device:TPU:0, one launch (start us, length us, event | category | flops | bytes accessed | tf_op | source)
XLA Modules:
  0.0 35.1 jit_solution(13905372724366949926)
XLA Ops:
  0.6 31.7 %cg.1 = (f32[48,8,1024]{2,1,0:T(8,128)S(1)}, f32[1,1]{1,0:T(1,128)}) custom-call(s32[48,8,1024]{2,1,0:T(8,128)} %signs_hbm.1, s32[8,1024]{1,0:T(8,128)} %mask_ref.1, f32[8,1024]{1,0:T(8,128)} %weight_ref.1, f32[8,1024]{1,0:T(8,128)} %prior_ref.1), custom_call_target="tpu_custom_call" | custom-call | tf_op jit(solution)/shard_map/cg/pallas_call | solution.py:413
  32.3 1.1 %copy.8 = f32[48,8,1024]{2,1,0:T(8,128)} copy(f32[48,8,1024]{2,1,0:T(8,128)S(1)} %get-tuple-element.6) | data formatting | bytes 3145728

commit v4 on v3

--- a/solution.py
+++ b/solution.py
@@ -154,10 +154,13 @@
     meet(barrier, 1)
     for bit in range(probe_bits):
         pl.semaphore_signal(barrier, 1, device_id=(flip(bit), space), device_id_type=MESH)
-    loads = pltpu.make_async_copy(signs_hbm, signs, load_sem)
-    loads.start()
+    def load(c):
+        at = pl.ds(c * chunk, chunk)
+        return pltpu.make_async_copy(signs_hbm.at[at], signs.at[at], load_sem.at[c])
+
+    for c in range(chunks):
+        load(c).start()
     diag[...] = mask_ref[...].astype(jnp.float32) * weight_ref[...] + prior_ref[...]
-    loads.wait()
     pl.semaphore_wait(barrier, met(1) + probe_bits)
 
     def pieces(stage):
@@ -188,6 +191,8 @@
             diag_copy(side).start()
     for stage in (0, 1):
         for c in range(chunks):
+            if stage == 0:
+                load(c).wait()
             for side, there in ((0, has_prev), (1, has_next)):
                 @pl.when(there)
                 def _():
@@ -404,7 +409,7 @@
 
     def on_device(probe_signs, sensor_mask, sensor_weight, prior_mass):
         probes, rows, cols = probe_signs.shape
-        chunk = next(c for c in (8, 6, 4, 3, 2, 1) if probes % c == 0)
+        chunk = next(c for c in (12, 8, 6, 4, 3, 2, 1) if probes % c == 0)
         chunks = probes // chunk
         full = (probes, rows, cols)
         dma, regular = pltpu.SemaphoreType.DMA, lambda n: pltpu.SemaphoreType.REGULAR(n)
@@ -425,7 +430,7 @@
                 pltpu.VMEM((2, 8, LANES), f32), pltpu.VMEM((2, space_n, 8, LANES), f32),
                 pltpu.VMEM((8, LANES), f32), pltpu.VMEM((probe_n, 8, LANES), f32),
                 pltpu.VMEM((8, probes, LANES), f32),
-                dma, dma((2,)), dma((2,)),
+                dma((chunks,)), dma((2,)), dma((2,)),
                 dma((2, 2, chunks)), dma((2, 2, chunks)),
                 dma((2, space_n)), dma((2, space_n)), dma((probe_n,)), dma((probe_n,)),
                 regular((8,)), regular((8, 8)),

time: 35.4 us -> 34.6 us (0.977)
  Pallas kernels: 31.7 us -> 30.9 us
    pallas_call x1, Pallas kernels: 31.7 us -> 30.9 us  [on_device(): pl.pallas_call(functools.partial(kernel, ('probe', 'space'), chunk), out_...]
where the time goes in v4:
time: 34.6 us; the launch traced here: 34.4 us
  Pallas kernels  30.9 us (89%)
  between operations  2.33 us (7%)
  local copies, waits for them, and re-layouts  1.15 us (3%)
    pallas_call x1, Pallas kernels, on_device(): pl.pallas_call(functools.partial(kernel, ('probe', 'space'), chunk), out_...  30.9 us
    unnamed x1, local copies, waits for them, and re-layouts  1.15 us

profile of v4, /device:TPU:0, one launch (start us, length us, event | category | flops | bytes accessed | tf_op | source)
XLA Modules:
  0.0 34.4 jit_solution(14096982518977717528)
XLA Ops:
  0.6 30.9 %cg.1 = (f32[48,8,1024]{2,1,0:T(8,128)S(1)}, f32[1,1]{1,0:T(1,128)}) custom-call(s32[48,8,1024]{2,1,0:T(8,128)} %signs_hbm.1, s32[8,1024]{1,0:T(8,128)} %mask_ref.1, f32[8,1024]{1,0:T(8,128)} %weight_ref.1, f32[8,1024]{1,0:T(8,128)} %prior_ref.1), custom_call_target="tpu_custom_call" | custom-call | tf_op jit(solution)/shard_map/cg/pallas_call | solution.py:418
  31.6 1.1 %copy.8 = f32[48,8,1024]{2,1,0:T(8,128)} copy(f32[48,8,1024]{2,1,0:T(8,128)S(1)} %get-tuple-element.6) | data formatting | bytes 3145728
